TPU v7x, 32 devices: a whole 2x2x4 slice. The times are simulated.
32 devices in a mesh: dp: 2 (over x), expert: 16 (over z, y, core).
Axes of the slice: x: 2, y: 2, z: 4, core: 2. Of those that a mesh axis runs over, the one named last changes fastest.
Arguments:
- tokens: bfloat16 [4096, 1024], P(('dp', 'expert')), may hold values from -6 to 6
- out_grad: bfloat16 [4096, 1024], P(('dp', 'expert')), may hold values from -6 to 6
- expert_ids: int32 [4096, 3], P(('dp', 'expert')), may hold values from 0 to 15, all different within a row; in each aligned block of 128 rows (0 to 127, 128 to 255, ...) at most 30 rows name the same one
- gate_probs: float32 [4096, 3], P(('dp', 'expert')), may hold values from 0.1 to 0.6
- saved_pre: bfloat16 [2, 16, 480, 1536], P('dp', 'expert'), may hold values from -6 to 6
- gate_weight: bfloat16 [16, 1024, 768], P('expert', 'dp'), may hold values from -0.1875 to 0.1875
- up_weight: bfloat16 [16, 1024, 768], P('expert', 'dp'), may hold values from -0.1875 to 0.1875
- down_weight: bfloat16 [16, 1024, 768], P('expert', 'dp'), may hold values from -0.21875 to 0.21875
- basis: bfloat16 [16, 1024, 256], P('expert', 'dp'), may hold values from -0.1875 to 0.1875
Outputs:
- in_grad: bfloat16 [4096, 1024], P(('dp', 'expert'))
- proj_grads: float32 [16, 3, 256, 768], P('expert', None, 'dp')
Inputs may be any that keep to these rules, and one draw needn't show every extreme that they name: `expert_ids`: each token names 3 different experts. The rows of one device name one expert at most 30 times, and on some devices some expert exactly 30 times.
All inputs are finite; a program needn't handle non-finite values.
Results may differ from a plain program's by a relative error of at most 0.0091.
Values may be sent and summed in bfloat16 or wider, within the bound.
A program may use at most 64 MiB of HBM per device.

v0:
```python
import jax
import jax.numpy as jnp
from jax import lax
from jax.sharding import PartitionSpec as P


def contract_rows(left, right):
    return lax.dot_general(
        left, right, (((0,), (0,)), ((), ())), preferred_element_type=jnp.float32
    )


def contract_cols(left, right):
    return lax.dot_general(
        left, right, (((1,), (1,)), ((), ())), preferred_element_type=jnp.float32
    )


def body(
    tokens, out_grad, expert_ids, gate_probs, saved_pre, gate_weight, up_weight, down_weight, basis
):
    n_owner = lax.axis_size("expert")
    tok_rows, width = tokens.shape
    topk = expert_ids.shape[1]
    slots = saved_pre.shape[2]
    cap = slots // n_owner
    hidden = gate_weight.shape[2]
    onehot = (expert_ids[:, :, None] == jnp.arange(n_owner, dtype=jnp.int32)[None, None, :]).astype(
        jnp.int32
    )
    per_token = jnp.sum(onehot, axis=1)
    before = jnp.cumsum(per_token, axis=0) - per_token
    position = jnp.sum(onehot * before[:, None, :], axis=2)
    target = expert_ids * cap + position
    token_index = jnp.broadcast_to(jnp.arange(tok_rows, dtype=jnp.int32)[:, None], target.shape)
    choice_index = jnp.broadcast_to(jnp.arange(topk, dtype=jnp.int32)[None, :], target.shape)
    fill_token = (
        jnp.full((n_owner * cap,), -1, jnp.int32)
        .at[target.reshape(-1)]
        .set(token_index.reshape(-1))
    )
    fill_choice = (
        jnp.zeros((n_owner * cap,), jnp.int32).at[target.reshape(-1)].set(choice_index.reshape(-1))
    )
    filled = fill_token >= 0
    picked = jnp.maximum(fill_token, 0)
    send_rows = jnp.where(filled[:, None], tokens[picked], jnp.zeros((), jnp.bfloat16))
    weight_pick = gate_probs[picked, fill_choice]
    scaled = (out_grad[picked].astype(jnp.float32) * weight_pick[:, None]).astype(jnp.bfloat16)
    send_grad = jnp.where(filled[:, None], scaled, jnp.zeros((), jnp.bfloat16))
    arrived_rows, arrived_grad = (
        lax.all_to_all(
            send_rows.reshape(n_owner, cap, width),
            "expert",
            split_axis=0,
            concat_axis=0,
            tiled=True,
        ),
        lax.all_to_all(
            send_grad.reshape(n_owner, cap, width),
            "expert",
            split_axis=0,
            concat_axis=0,
            tiled=True,
        ),
    )
    rows_in = arrived_rows.reshape(slots, width)
    grad_in = arrived_grad.reshape(slots, width)
    pieces = (
        lax.all_gather(down_weight, "dp", axis=1, tiled=True),
        lax.all_gather(basis, "dp", axis=1, tiled=True),
    )
    down_piece = pieces[0][0]
    basis_piece = pieces[1][0]
    hidden_grad = jnp.dot(grad_in, down_piece, preferred_element_type=jnp.float32)
    x_acc = jnp.dot(rows_in, basis_piece, preferred_element_type=jnp.float32)
    dy_acc = jnp.dot(grad_in, basis_piece, preferred_element_type=jnp.float32)
    hidden_grad, x_acc, dy_acc = (hidden_grad, x_acc, dy_acc)
    pre = saved_pre[0, 0].astype(jnp.float32)
    gate_pre = pre[:, :hidden]
    up_pre = pre[:, hidden:]
    sig = jax.nn.sigmoid(gate_pre)
    hid = (gate_pre * sig * up_pre).astype(jnp.bfloat16)
    up_grad = (hidden_grad * gate_pre * sig).astype(jnp.bfloat16)
    gate_grad = (hidden_grad * up_pre * sig * (1.0 + gate_pre * (1.0 - sig))).astype(jnp.bfloat16)
    x_proj = x_acc.astype(jnp.bfloat16)
    dy_proj = dy_acc.astype(jnp.bfloat16)
    pieces = lax.all_gather((gate_weight, up_weight), "dp", axis=1, tiled=True)
    row_grad = contract_cols(gate_grad, pieces[0][0]) + contract_cols(up_grad, pieces[1][0])
    terms = jnp.stack(
        [
            contract_rows(x_proj, gate_grad),
            contract_rows(x_proj, up_grad),
            contract_rows(dy_proj, hid),
        ]
    )
    proj_grads = lax.psum_scatter(terms[None], "dp", scatter_dimension=2, tiled=True)
    returned = lax.all_to_all(
        row_grad.astype(jnp.bfloat16).reshape(n_owner, cap, width),
        "expert",
        split_axis=0,
        concat_axis=0,
        tiled=True,
    )
    returned = returned.reshape(n_owner * cap, width)
    in_grad = jnp.sum(returned[target].astype(jnp.float32), axis=1).astype(jnp.bfloat16)
    return (in_grad, proj_grads)


def solution(mesh):
    return jax.shard_map(
        body,
        mesh=mesh,
        in_specs=(
            P(("dp", "expert"), None),
            P(("dp", "expert"), None),
            P(("dp", "expert"), None),
            P(("dp", "expert"), None),
            P("dp", "expert", None, None),
            P("expert", "dp", None),
            P("expert", "dp", None),
            P("expert", "dp", None),
            P("expert", "dp", None),
        ),
        out_specs=(P(("dp", "expert"), None), P("expert", None, "dp", None)),
        check_vma=False,
    )
```

profile of v0, /device:TPU:11, one launch (start us, length us, event | category | flops | bytes accessed | tf_op | source)
XLA Modules:
  0.0 154.2 jit_solution(18222967836924440757)
XLA Ops:
  11.1 2.9 %scatter_custom_fusion.1 = s32[480]{0:T(512)S(1)} fusion(s32[384]{0:T(512)S(1)} %fusion.12, s32[384]{0:T(512)S(1)} %reshape.139, s32[]{:T(128)} %constant.9.clone.1), kind=kCustom, calls=%fused_computation.41 | custom fusion | bytes 1924 | tf_op jit(solution)/shard_map/scatter | solution.py:43
  14.1 2.9 %scatter_custom_fusion = s32[480]{0:T(512)S(1)} fusion(s32[384]{0:T(512)S(1)} %fusion.12, s32[384]{0:T(512)S(1)} %reshape.131, s32[]{:T(128)} %constant.7.clone.1), kind=kCustom, calls=%fused_computation.45 | custom fusion | bytes 1924 | tf_op jit(solution)/shard_map/scatter | solution.py:40
  17.0 2.8 %gather_fusion = bf16[480,1024]{1,0:T(8,128)(2,1)} fusion(bf16[128,1024]{1,0:T(8,128)(2,1)S(1)} %copy-done, s32[1024]{0:T(1024)S(1)} %pad_clamp_fusion.1), kind=kCustom, calls=%fused_computation | custom fusion | bytes 1968000 | tf_op jit(solution)/shard_map/gather | solution.py:49
  19.8 1.5 reshape.95
  21.3 2.8 %gather_fusion.3 = bf16[480,1024]{1,0:T(8,128)(2,1)} fusion(bf16[128,1024]{1,0:T(8,128)(2,1)S(1)} %copy-done.2, s32[1024]{0:T(1024)S(1)} %pad_clamp_fusion.1), kind=kCustom, calls=%fused_computation.3 | custom fusion | bytes 1968000 | tf_op jit(solution)/shard_map/gather | solution.py:47
  24.1 1.4 gather.18
  25.5 4.6 %gather_fusion.1 = f32[480]{0:T(512)S(1)} fusion(f32[128,3]{0,1:T(4,128)S(1)} %copy-done.1, s32[480]{0:T(512)S(1)} %get-tuple-element.8), kind=kCustom, calls=%fused_computation.1 | custom fusion | bytes 7680 | tf_op jit(solution)/shard_map/gather | solution.py:48
  30.3 1.7 %broadcast_select_fusion = (bf16[16,30,1024]{2,1,0:T(8,128)(2,1)}, bf16[16,30,1024]{2,1,0:T(8,128)(2,1)}) fusion(bf16[16,30,1024]{2,1,0:T(8,128)(2,1)S(1)} %gather.18, pred[16,30]{1,0:T(8,128)(4,1)S(1)} %broadcast_in_dim.57, f32[16,30,1024]{2,1,0:T(8,128)S(1)} %reshape.95, f32[16,30]{1,0:T(8,128)S(1)} %mul.53), kind=kLoop, calls=%fused_computation.25 | loop fusion | flops 1966080 | bytes 4917600 | tf_op jit(solution)/shard_map/jit(_where)/select_n | solution.py:47
  32.0 6.5 %all-to-all-start.2 = ((bf16[16,30,1024]{2,1,0:T(8,128)(2,1)}), bf16[16,30,1024]{2,1,0:T(8,128)(2,1)S(1)}, u32[]{:S(2)}, u32[]{:S(2)}) async-start(bf16[16,30,1024]{2,1,0:T(8,128)(2,1)} %get-tuple-element.6), calls=%async_computation.2 | async-start | bytes 2097152 | tf_op jit(solution)/shard_map/all_to_all | solution.py:52
  39.3 24.2 %all-to-all-done.2 = bf16[16,30,1024]{2,1,0:T(8,128)(2,1)S(1)} async-done(((bf16[16,30,1024]{2,1,0:T(8,128)(2,1)}), bf16[16,30,1024]{2,1,0:T(8,128)(2,1)S(1)}, u32[]{:S(2)}, u32[]{:S(2)}) %all-to-all-start.2) | async-done | bytes 983072 | tf_op jit(solution)/shard_map/all_to_all | solution.py:52
  63.5 4.7 %all-to-all-start = ((bf16[16,30,1024]{2,1,0:T(8,128)(2,1)}), bf16[16,30,1024]{2,1,0:T(8,128)(2,1)S(1)}, u32[]{:S(2)}, u32[]{:S(2)}) async-start(bf16[16,30,1024]{2,1,0:T(8,128)(2,1)} %get-tuple-element.7), calls=%async_computation | async-start | bytes 2097152 | tf_op jit(solution)/shard_map/all_to_all | solution.py:59
  69.0 8.3 %all_gather.15 = bf16[1,1024,256]{2,1,0:T(8,128)(2,1)S(1)} all-gather(bf16[1,512,256]{2,1,0:T(8,128)(2,1)S(1)} %copy-done.7), channel_id=1, replica_groups=mesh['dp'=2,'expert'=16] {'dp'}, dimensions={1}, use_global_device_ids=true | all-gather | bytes 786432 | tf_op jit(solution)/shard_map/all_gather | solution.py:71
  77.4 3.7 %bitcast_convert_fusion = f32[480,1536]{1,0:T(8,128)} fusion(bf16[1,1,480,1536]{3,2,1,0:T(8,128)(2,1)} %param.13), kind=kLoop, calls=%fused_computation.14 | loop fusion | flops 737280 | bytes 4423680 | tf_op jit(solution)/shard_map/convert_element_type | solution.py:79
  82.2 1.6 %convolution_convert_fusion.1 = bf16[480,256]{1,0:T(8,128)(2,1)S(1)} fusion(bf16[480,1024]{1,0:T(8,128)(2,1)} %reshape.94, bf16[1,1024,256]{2,1,0:T(8,128)(2,1)S(1)} %all_gather.15), kind=kOutput, calls=%fused_computation.23 | convolution fusion | flops 251781120 | bytes 1753088 | tf_op jit(solution)/shard_map/dot_general | solution.py:76
  83.8 9.4 %all-to-all-done = bf16[16,30,1024]{2,1,0:T(8,128)(2,1)S(1)} async-done(((bf16[16,30,1024]{2,1,0:T(8,128)(2,1)}), bf16[16,30,1024]{2,1,0:T(8,128)(2,1)S(1)}, u32[]{:S(2)}, u32[]{:S(2)}) %all-to-all-start) | async-done | bytes 983072 | tf_op jit(solution)/shard_map/all_to_all | solution.py:59
  93.5 3.8 %multiply_convert_fusion.2 = (bf16[480,768]{1,0:T(8,128)(2,1)S(1)}, bf16[480,768]{1,0:T(8,128)(2,1)S(1)}) fusion(f32[480,1536]{1,0:T(8,128)} %bitcast_convert_fusion, bf16[480,1024]{1,0:T(8,128)(2,1)S(1)} %reshape.91, bf16[1,1024,768]{2,1,0:T(8,128)(2,1)} %all-gather.4.cloned.1.call-done), kind=kOutput, calls=%fused_computation.16 | convolution fusion | flops 759767040 | bytes 6979584 | tf_op jit(solution)/shard_map/dot_general | solution.py:75
  98.7 3.4 %convolution_bitcast_fusion = f32[1,256,768]{2,1,0:T(8,128)S(1)} fusion(bf16[480,1024]{1,0:T(8,128)(2,1)} %copy-done.3, f32[480,1536]{1,0:T(8,128)} %bitcast_convert_fusion, bf16[1,1024,256]{2,1,0:T(8,128)(2,1)} %copy-done.6), kind=kOutput, calls=%fused_computation.19 | convolution fusion | flops 442736640 | bytes 5242880 | tf_op jit(solution)/shard_map/dot_general | solution.py:8
  102.1 1.6 %maximum_bitcast_fusion = f32[1,3,256,768]{3,2,1,0:T(8,128)} fusion(f32[1,256,768]{2,1,0:T(8,128)S(1)} %convolution_bitcast_fusion, f32[1,256,768]{2,1,0:T(8,128)S(1)} %convolution_bitcast_fusion.1, f32[1,256,768]{2,1,0:T(8,128)S(1)} %convolution_bitcast_fusion.2), kind=kLoop, calls=%fused_computation.6 | loop fusion | flops 1179648 | bytes 4718592 | tf_op jit(solution)/shard_map/broadcast_in_dim | solution.py:97
  104.8 3.7 %fusion.1 = f32[480,1024]{1,0:T(8,128)} fusion(bf16[480,768]{1,0:T(8,128)(2,1)S(1)} %copy-done.5, bf16[1,1024,768]{2,1,0:T(8,128)(2,1)} %all-gather.6.cloned.1.call-done), kind=kOutput, calls=%fused_computation.10 | convolution fusion | flops 754974720 | bytes 4276224 | tf_op jit(solution)/shard_map/dot_general | solution.py:14
  108.5 3.6 %add_convert_fusion = bf16[480,1024]{1,0:T(8,128)(2,1)S(1)} fusion(f32[480,1024]{1,0:T(8,128)} %fusion.1, bf16[480,768]{1,0:T(8,128)(2,1)S(1)} %get-tuple-element.4, bf16[1,1024,768]{2,1,0:T(8,128)(2,1)} %all-gather.8.cloned.1.call-done), kind=kOutput, calls=%fused_computation.8 | convolution fusion | flops 755957760 | bytes 5259264 | tf_op jit(solution)/shard_map/dot_general | solution.py:14
  113.4 4.5 %all-to-all-start.1 = ((bf16[16,30,1024]{2,1,0:T(8,128)(2,1)}), bf16[16,30,1024]{2,1,0:T(8,128)(2,1)S(1)}, u32[]{:S(2)}, u32[]{:S(2)}) async-start(bf16[16,30,1024]{2,1,0:T(8,128)(2,1)} %reshape.92), calls=%async_computation.1 | async-start | bytes 2097152 | tf_op jit(solution)/shard_map/all_to_all | solution.py:98
  118.2 24.6 %all-to-all-done.1 = bf16[16,30,1024]{2,1,0:T(8,128)(2,1)S(1)} async-done(((bf16[16,30,1024]{2,1,0:T(8,128)(2,1)}), bf16[16,30,1024]{2,1,0:T(8,128)(2,1)S(1)}, u32[]{:S(2)}, u32[]{:S(2)}) %all-to-all-start.1) | async-done | bytes 983072 | tf_op jit(solution)/shard_map/all_to_all | solution.py:98
  143.0 2.1 %gather_fusion.2 = bf16[384,1024]{1,0:T(8,128)(2,1)S(1)} fusion(bf16[480,1024]{1,0:T(8,128)(2,1)S(1)} %reshape.93, s32[1024]{0:T(1024)S(1)} %pad_clamp_fusion), kind=kCustom, calls=%fused_computation.2 | custom fusion | bytes 1574400 | tf_op jit(solution)/shard_map/gather | solution.py:106
  145.6 2.1 %reduce_sum.32 = bf16[128,1024]{1,0:T(8,128)(2,1)} reduce(bf16[128,3,1024]{2,1,0:T(4,128)(2,1)S(1)} %reshape.116, bf16[]{:T(256)} %constant.12.clone.1), dimensions={1}, to_apply=%region_5.6 | reduce | flops 262144 | bytes 1048578 | tf_op jit(solution)/shard_map/reduce_sum | solution.py:106
  (57 shorter events, 11.8 us)
Async XLA Ops:
  7.2 9.9 %copy-start = (bf16[128,1024]{1,0:T(8,128)(2,1)S(1)}, bf16[128,1024]{1,0:T(8,128)(2,1)}, u32[]{:S(2)}) copy-start(bf16[128,1024]{1,0:T(8,128)(2,1)} %param.10) | copy-start | bytes 786436
  7.2 86.3 %all-gather.4.cloned.1.call-start = ((), (), s32[]{:S(2)}) async-start(), calls=%async_computation.4 | async-start | bytes 2359296 | tf_op jit(solution)/shard_map/all_gather | solution.py:70
  19.8 1.5 copy-start.2
  24.1 1.5 copy-start.1
  32.0 31.5 %all-to-all-start.2 = ((bf16[16,30,1024]{2,1,0:T(8,128)(2,1)}), bf16[16,30,1024]{2,1,0:T(8,128)(2,1)S(1)}, u32[]{:S(2)}, u32[]{:S(2)}) async-start(bf16[16,30,1024]{2,1,0:T(8,128)(2,1)} %get-tuple-element.6), calls=%async_computation.2 | async-start | bytes 2097152 | tf_op jit(solution)/shard_map/all_to_all | solution.py:52
  38.6 65.2 %all-gather.6.cloned.1.call-start = ((), (), s32[]{:S(2)}) async-start(), calls=%async_computation.5 | async-start | bytes 2359296 | tf_op jit(solution)/shard_map/all_gather | solution.py:88
  39.3 29.7 %copy-start.7 = (bf16[1,512,256]{2,1,0:T(8,128)(2,1)S(1)}, bf16[1,512,256]{2,1,0:T(8,128)(2,1)}, u32[]{:S(2)}) copy-start(bf16[1,512,256]{2,1,0:T(8,128)(2,1)} %param.17) | copy-start | bytes 786436
  63.5 29.7 %all-to-all-start = ((bf16[16,30,1024]{2,1,0:T(8,128)(2,1)}), bf16[16,30,1024]{2,1,0:T(8,128)(2,1)S(1)}, u32[]{:S(2)}, u32[]{:S(2)}) async-start(bf16[16,30,1024]{2,1,0:T(8,128)(2,1)} %get-tuple-element.7), calls=%async_computation | async-start | bytes 2097152 | tf_op jit(solution)/shard_map/all_to_all | solution.py:59
  68.2 40.2 %all-gather.8.cloned.1.call-start = ((), (), s32[]{:S(2)}) async-start(), calls=%async_computation.6 | async-start | bytes 2359296 | tf_op jit(solution)/shard_map/all_gather | solution.py:88
  69.0 78.7 %reduce-scatter.2.cloned.1.call-start = ((), (), s32[]{:S(2)}) async-start(), calls=%async_computation.7 | async-start | bytes 3538944 | tf_op jit(solution)/shard_map/reduce_scatter | solution.py:97
  77.3 4.9 %copy-start.6 = (bf16[1,1024,256]{2,1,0:T(8,128)(2,1)}, bf16[1,1024,256]{2,1,0:T(8,128)(2,1)S(1)}, u32[]{:S(2)}) copy-start(bf16[1,1024,256]{2,1,0:T(8,128)(2,1)S(1)} %all_gather.15) | copy-start | bytes 1572868
  93.5 3.9 %copy-start.3 = (bf16[480,1024]{1,0:T(8,128)(2,1)}, bf16[480,1024]{1,0:T(8,128)(2,1)S(1)}, u32[]{:S(2)}) copy-start(bf16[480,1024]{1,0:T(8,128)(2,1)S(1)} %reshape.91) | copy-start | bytes 2949124
  97.4 0.9 copy-start.4
  103.7 1.1 copy-start.5
  113.4 29.4 %all-to-all-start.1 = ((bf16[16,30,1024]{2,1,0:T(8,128)(2,1)}), bf16[16,30,1024]{2,1,0:T(8,128)(2,1)S(1)}, u32[]{:S(2)}, u32[]{:S(2)}) async-start(bf16[16,30,1024]{2,1,0:T(8,128)(2,1)} %reshape.92), calls=%async_computation.1 | async-start | bytes 2097152 | tf_op jit(solution)/shard_map/all_to_all | solution.py:98
Sparse Core Ops, SparseCore 0:
  9.5 27.2 all-gather.3
  40.9 26.6 all-gather.5
  70.6 26.6 all-gather.7
  103.9 33.0 reduce-scatter.1
where the time goes:
time: 155 us; the launch traced here: 154 us
  waiting for transfers between devices  60.3 us (39%)
  local copies, waits for them, and re-layouts  27.4 us (18%)
  matrix products  16.9 us (11%)
  starting transfers between devices  15.8 us (10%)
  between operations  14 us (9%)
  other arithmetic  11.4 us (7%)
  blocking collectives  8.31 us (5%)
    all_to_all x1, waiting for transfers between devices, body(): lax.all_to_all(row_grad.astype(jnp.bfloat16).reshape(n_owner, cap, width)...  24.6 us
    all_to_all x1, waiting for transfers between devices, body(): lax.all_to_all(send_rows.reshape(n_owner, cap, width), 'expert', split_ax...  24.2 us
    all_to_all x1, waiting for transfers between devices, body(): lax.all_to_all(send_grad.reshape(n_owner, cap, width), 'expert', split_ax...  9.38 us
    all_gather x1, blocking collectives, body(): lax.all_gather(basis, 'dp', axis=1, tiled=True)  8.31 us
    dot_general x2, matrix products, contract_cols(): lax.dot_general(left, right, (((1,), (1,)), ((), ())), preferred_element_...  7.29 us
    all_to_all x1, starting transfers between devices, body(): lax.all_to_all(send_rows.reshape(n_owner, cap, width), 'expert', split_ax...  6.52 us
    all_to_all x1, starting transfers between devices, body(): lax.all_to_all(send_grad.reshape(n_owner, cap, width), 'expert', split_ax...  4.7 us
    gather x1, local copies, waits for them, and re-layouts, body(): weight_pick = gate_probs[picked, fill_choice]  4.64 us
  transfers between devices with their start and end apart: 7, of which 3 were waited for; matrix products, arithmetic and copies ran while one was open for 35% of the time, Pallas kernels for 0%

commit v1 on v0

--- a/solution.py
+++ b/solution.py
@@ -2,6 +2,18 @@
 import jax.numpy as jnp
 from jax import lax
 from jax.sharding import PartitionSpec as P
+
+
+def collect(array, axis, dim):
+    ways, here, turn = (lax.axis_size(axis), lax.axis_index(axis), array.shape[dim])
+    line, have = (array, 1)
+    while have < ways:
+        line = jnp.concatenate(
+            [line, lax.ppermute(line, axis, [(d, (d - have) % ways) for d in range(ways)])],
+            axis=dim,
+        )
+        have = 2 * have
+    return jnp.roll(line, here * turn, axis=dim)
 
 
 def contract_rows(left, right):
@@ -66,10 +78,7 @@
     )
     rows_in = arrived_rows.reshape(slots, width)
     grad_in = arrived_grad.reshape(slots, width)
-    pieces = (
-        lax.all_gather(down_weight, "dp", axis=1, tiled=True),
-        lax.all_gather(basis, "dp", axis=1, tiled=True),
-    )
+    pieces = (lax.all_gather(down_weight, "dp", axis=1, tiled=True), collect(basis, "dp", 1))
     down_piece = pieces[0][0]
     basis_piece = pieces[1][0]
     hidden_grad = jnp.dot(grad_in, down_piece, preferred_element_type=jnp.float32)

time: 155 us -> 155 us (level)
  blocking collectives: 8.31 us -> 0 us
  waiting for transfers between devices: 60.3 us -> 65.9 us
  other arithmetic: 11.4 us -> 13.4 us
    all_gather x1 -> x0, blocking collectives: 8.31 us -> none  [body(): lax.all_gather(basis, 'dp', axis=1, tiled=True)]
    ppermute x0 -> x1, waiting for transfers between devices: none -> 3.36 us  [collect(): lax.ppermute(line, axis, [(d, (d - have) % ways) for d in range(ways)])]
    all_to_all x1, waiting for transfers between devices: 9.38 us -> 11.9 us  [body(): lax.all_to_all(send_grad.reshape(n_owner, cap, width), 'expert', split_ax...]
    squeeze x0 -> x1, other arithmetic: none -> 2.41 us  [body(): basis_piece = pieces[1][0]]
  transfers between devices with their start and end apart: 7 -> 8, of which waited for: 3 -> 4; matrix products, arithmetic and copies ran while one was open for 35% -> 36% of each run, Pallas kernels for 0% -> 0%
where the time goes in v1:
time: 155 us; the launch traced here: 154 us
  waiting for transfers between devices  65.9 us (43%)
  local copies, waits for them, and re-layouts  27.4 us (18%)
  matrix products  17 us (11%)
  starting transfers between devices  16.4 us (11%)
  between operations  14 us (9%)
  other arithmetic  13.4 us (9%)
    all_to_all x1, waiting for transfers between devices, body(): lax.all_to_all(row_grad.astype(jnp.bfloat16).reshape(n_owner, cap, width)...  24.6 us
    all_to_all x1, waiting for transfers between devices, body(): lax.all_to_all(send_rows.reshape(n_owner, cap, width), 'expert', split_ax...  24.2 us
    all_to_all x1, waiting for transfers between devices, body(): lax.all_to_all(send_grad.reshape(n_owner, cap, width), 'expert', split_ax...  11.9 us
    dot_general x2, matrix products, contract_cols(): lax.dot_general(left, right, (((1,), (1,)), ((), ())), preferred_element_...  7.28 us
    all_to_all x1, starting transfers between devices, body(): lax.all_to_all(send_rows.reshape(n_owner, cap, width), 'expert', split_ax...  6.52 us
    all_to_all x1, starting transfers between devices, body(): lax.all_to_all(send_grad.reshape(n_owner, cap, width), 'expert', split_ax...  4.7 us
    gather x1, local copies, waits for them, and re-layouts, body(): weight_pick = gate_probs[picked, fill_choice]  4.64 us
    all_to_all x1, starting transfers between devices, body(): lax.all_to_all(row_grad.astype(jnp.bfloat16).reshape(n_owner, cap, width)...  4.48 us
  transfers between devices with their start and end apart: 8, of which 4 were waited for; matrix products, arithmetic and copies ran while one was open for 36% of the time, Pallas kernels for 0%

profile of v1, /device:TPU:11, one launch (start us, length us, event | category | flops | bytes accessed | tf_op | source)
XLA Modules:
  0.0 154.0 jit_solution(10189750230395397855)
XLA Ops:
  11.1 2.9 %scatter_custom_fusion.1 = s32[480]{0:T(512)S(1)} fusion(s32[384]{0:T(512)S(1)} %fusion.13, s32[384]{0:T(512)S(1)} %reshape.139, s32[]{:T(128)} %constant.44.clone.1), kind=kCustom, calls=%fused_computation.47 | custom fusion | bytes 1924 | tf_op jit(solution)/shard_map/scatter | solution.py:55
  14.1 2.9 %scatter_custom_fusion = s32[480]{0:T(512)S(1)} fusion(s32[384]{0:T(512)S(1)} %fusion.13, s32[384]{0:T(512)S(1)} %reshape.131, s32[]{:T(128)} %constant.21.clone.1), kind=kCustom, calls=%fused_computation.51 | custom fusion | bytes 1924 | tf_op jit(solution)/shard_map/scatter | solution.py:52
  17.0 2.8 %gather_fusion = bf16[480,1024]{1,0:T(8,128)(2,1)} fusion(bf16[128,1024]{1,0:T(8,128)(2,1)S(1)} %copy-done, s32[1024]{0:T(1024)S(1)} %pad_clamp_fusion.1), kind=kCustom, calls=%fused_computation | custom fusion | bytes 1968000 | tf_op jit(solution)/shard_map/gather | solution.py:61
  19.8 1.5 reshape.95
  21.3 2.8 %gather_fusion.3 = bf16[480,1024]{1,0:T(8,128)(2,1)} fusion(bf16[128,1024]{1,0:T(8,128)(2,1)S(1)} %copy-done.2, s32[1024]{0:T(1024)S(1)} %pad_clamp_fusion.1), kind=kCustom, calls=%fused_computation.3 | custom fusion | bytes 1968000 | tf_op jit(solution)/shard_map/gather | solution.py:59
  25.5 4.6 %gather_fusion.1 = f32[480]{0:T(512)S(1)} fusion(f32[128,3]{0,1:T(4,128)S(1)} %copy-done.1, s32[480]{0:T(512)S(1)} %get-tuple-element.8), kind=kCustom, calls=%fused_computation.1 | custom fusion | bytes 7680 | tf_op jit(solution)/shard_map/gather | solution.py:60
  30.3 1.6 %broadcast_select_fusion = (bf16[16,30,1024]{2,1,0:T(8,128)(2,1)}, bf16[16,30,1024]{2,1,0:T(8,128)(2,1)}) fusion(bf16[16,30,1024]{2,1,0:T(8,128)(2,1)S(1)} %gather.18, pred[16,30]{1,0:T(8,128)(4,1)S(1)} %broadcast_in_dim.57, f32[16,30,1024]{2,1,0:T(8,128)S(1)} %reshape.95, f32[16,30]{1,0:T(8,128)S(1)} %mul.56), kind=kLoop, calls=%fused_computation.29 | loop fusion | flops 1966080 | bytes 4917600 | tf_op jit(solution)/shard_map/jit(_where)/select_n | solution.py:59
  31.9 6.5 %all-to-all-start.2 = ((bf16[16,30,1024]{2,1,0:T(8,128)(2,1)}), bf16[16,30,1024]{2,1,0:T(8,128)(2,1)S(1)}, u32[]{:S(2)}, u32[]{:S(2)}) async-start(bf16[16,30,1024]{2,1,0:T(8,128)(2,1)} %get-tuple-element.6), calls=%async_computation.2 | async-start | bytes 2097152 | tf_op jit(solution)/shard_map/all_to_all | solution.py:64
  39.2 24.2 %all-to-all-done.2 = bf16[16,30,1024]{2,1,0:T(8,128)(2,1)S(1)} async-done(((bf16[16,30,1024]{2,1,0:T(8,128)(2,1)}), bf16[16,30,1024]{2,1,0:T(8,128)(2,1)S(1)}, u32[]{:S(2)}, u32[]{:S(2)}) %all-to-all-start.2) | async-done | bytes 983072 | tf_op jit(solution)/shard_map/all_to_all | solution.py:64
  63.4 4.7 %all-to-all-start = ((bf16[16,30,1024]{2,1,0:T(8,128)(2,1)}), bf16[16,30,1024]{2,1,0:T(8,128)(2,1)S(1)}, u32[]{:S(2)}, u32[]{:S(2)}) async-start(bf16[16,30,1024]{2,1,0:T(8,128)(2,1)} %get-tuple-element.7), calls=%async_computation | async-start | bytes 2097152 | tf_op jit(solution)/shard_map/all_to_all | solution.py:71
  69.1 3.4 %bitcast_convert_fusion = f32[480,1536]{1,0:T(8,128)} fusion(bf16[1,1,480,1536]{3,2,1,0:T(8,128)(2,1)} %param.13), kind=kLoop, calls=%fused_computation.14 | loop fusion | flops 737280 | bytes 4423680 | tf_op jit(solution)/shard_map/convert_element_type | solution.py:88
  72.5 3.4 %collective-permute-done = bf16[1,512,256]{2,1,0:T(8,128)(2,1)} collective-permute-done((bf16[1,512,256]{2,1,0:T(8,128)(2,1)S(1)}, bf16[1,512,256]{2,1,0:T(8,128)(2,1)}, u32[]{:S(2)}, u32[]{:S(2)}) %collective-permute-start) | collective-permute-done | bytes 262176 | tf_op jit(solution)/shard_map/ppermute | solution.py:12
  75.8 2.4 %fusion.9 = bf16[1024,256]{1,0:T(8,128)(2,1)S(1)} fusion(s32[]{:T(128)S(6)} %select_n.48, bf16[1,512,256]{2,1,0:T(8,128)(2,1)S(1)} %copy-done.7, bf16[1,512,256]{2,1,0:T(8,128)(2,1)} %collective-permute-done), kind=kLoop, calls=%fused_computation.33 | loop fusion | flops 2097152 | bytes 1048580 | tf_op jit(solution)/shard_map/squeeze | solution.py:83
  79.5 1.7 %convolution_convert_fusion.1 = bf16[480,256]{1,0:T(8,128)(2,1)S(1)} fusion(bf16[480,1024]{1,0:T(8,128)(2,1)} %reshape.94, bf16[1024,256]{1,0:T(8,128)(2,1)S(1)} %fusion.9), kind=kOutput, calls=%fused_computation.23 | convolution fusion | flops 251781120 | bytes 1753088 | tf_op jit(solution)/shard_map/dot_general | solution.py:85
  81.2 11.9 %all-to-all-done = bf16[16,30,1024]{2,1,0:T(8,128)(2,1)S(1)} async-done(((bf16[16,30,1024]{2,1,0:T(8,128)(2,1)}), bf16[16,30,1024]{2,1,0:T(8,128)(2,1)S(1)}, u32[]{:S(2)}, u32[]{:S(2)}) %all-to-all-start) | async-done | bytes 983072 | tf_op jit(solution)/shard_map/all_to_all | solution.py:71
  93.4 3.8 %multiply_convert_fusion.2 = (bf16[480,768]{1,0:T(8,128)(2,1)S(1)}, bf16[480,768]{1,0:T(8,128)(2,1)S(1)}) fusion(f32[480,1536]{1,0:T(8,128)} %bitcast_convert_fusion, bf16[480,1024]{1,0:T(8,128)(2,1)S(1)} %reshape.91, bf16[1,1024,768]{2,1,0:T(8,128)(2,1)} %all-gather.4.cloned.1.call-done), kind=kOutput, calls=%fused_computation.16 | convolution fusion | flops 759767040 | bytes 6979584 | tf_op jit(solution)/shard_map/dot_general | solution.py:84
  98.5 3.4 %convolution_bitcast_fusion = f32[1,256,768]{2,1,0:T(8,128)S(1)} fusion(bf16[480,1024]{1,0:T(8,128)(2,1)} %copy-done.3, bf16[1024,256]{1,0:T(8,128)(2,1)} %copy-done.6, f32[480,1536]{1,0:T(8,128)} %bitcast_convert_fusion), kind=kOutput, calls=%fused_computation.19 | convolution fusion | flops 442736640 | bytes 5242880 | tf_op jit(solution)/shard_map/dot_general | solution.py:20
  101.9 1.6 %maximum_bitcast_fusion = f32[1,3,256,768]{3,2,1,0:T(8,128)} fusion(f32[1,256,768]{2,1,0:T(8,128)S(1)} %convolution_bitcast_fusion, f32[1,256,768]{2,1,0:T(8,128)S(1)} %convolution_bitcast_fusion.1, f32[1,256,768]{2,1,0:T(8,128)S(1)} %convolution_bitcast_fusion.2), kind=kLoop, calls=%fused_computation.6 | loop fusion | flops 1179648 | bytes 4718592 | tf_op jit(solution)/shard_map/broadcast_in_dim | solution.py:106
  104.6 3.7 %fusion.1 = f32[480,1024]{1,0:T(8,128)} fusion(bf16[480,768]{1,0:T(8,128)(2,1)S(1)} %copy-done.5, bf16[1,1024,768]{2,1,0:T(8,128)(2,1)} %all-gather.6.cloned.1.call-done), kind=kOutput, calls=%fused_computation.10 | convolution fusion | flops 754974720 | bytes 4276224 | tf_op jit(solution)/shard_map/dot_general | solution.py:26
  108.3 3.6 %add_convert_fusion = bf16[480,1024]{1,0:T(8,128)(2,1)S(1)} fusion(f32[480,1024]{1,0:T(8,128)} %fusion.1, bf16[480,768]{1,0:T(8,128)(2,1)S(1)} %get-tuple-element.4, bf16[1,1024,768]{2,1,0:T(8,128)(2,1)} %all-gather.8.cloned.1.call-done), kind=kOutput, calls=%fused_computation.8 | convolution fusion | flops 755957760 | bytes 5259264 | tf_op jit(solution)/shard_map/dot_general | solution.py:26
  113.1 4.5 %all-to-all-start.1 = ((bf16[16,30,1024]{2,1,0:T(8,128)(2,1)}), bf16[16,30,1024]{2,1,0:T(8,128)(2,1)S(1)}, u32[]{:S(2)}, u32[]{:S(2)}) async-start(bf16[16,30,1024]{2,1,0:T(8,128)(2,1)} %reshape.92), calls=%async_computation.1 | async-start | bytes 2097152 | tf_op jit(solution)/shard_map/all_to_all | solution.py:107
  118.0 24.6 %all-to-all-done.1 = bf16[16,30,1024]{2,1,0:T(8,128)(2,1)S(1)} async-done(((bf16[16,30,1024]{2,1,0:T(8,128)(2,1)}), bf16[16,30,1024]{2,1,0:T(8,128)(2,1)S(1)}, u32[]{:S(2)}, u32[]{:S(2)}) %all-to-all-start.1) | async-done | bytes 983072 | tf_op jit(solution)/shard_map/all_to_all | solution.py:107
  142.8 2.1 %gather_fusion.2 = bf16[384,1024]{1,0:T(8,128)(2,1)S(1)} fusion(bf16[480,1024]{1,0:T(8,128)(2,1)S(1)} %reshape.93, s32[1024]{0:T(1024)S(1)} %pad_clamp_fusion), kind=kCustom, calls=%fused_computation.2 | custom fusion | bytes 1574400 | tf_op jit(solution)/shard_map/gather | solution.py:115
  145.4 2.1 %reduce_sum.32 = bf16[128,1024]{1,0:T(8,128)(2,1)} reduce(bf16[128,3,1024]{2,1,0:T(4,128)(2,1)S(1)} %reshape.116, bf16[]{:T(256)} %constant.47.clone.1), dimensions={1}, to_apply=%region_5.6 | reduce | flops 262144 | bytes 1048578 | tf_op jit(solution)/shard_map/reduce_sum | solution.py:115
  (59 shorter events, 13.4 us)
Async XLA Ops:
  7.2 9.9 %copy-start = (bf16[128,1024]{1,0:T(8,128)(2,1)S(1)}, bf16[128,1024]{1,0:T(8,128)(2,1)}, u32[]{:S(2)}) copy-start(bf16[128,1024]{1,0:T(8,128)(2,1)} %param.10) | copy-start | bytes 786436
  7.2 86.2 %all-gather.4.cloned.1.call-start = ((), (), s32[]{:S(2)}) async-start(), calls=%async_computation.4 | async-start | bytes 2359296 | tf_op jit(solution)/shard_map/all_gather | solution.py:81
  19.8 1.5 copy-start.2
  24.1 1.5 copy-start.1
  31.9 31.5 %all-to-all-start.2 = ((bf16[16,30,1024]{2,1,0:T(8,128)(2,1)}), bf16[16,30,1024]{2,1,0:T(8,128)(2,1)S(1)}, u32[]{:S(2)}, u32[]{:S(2)}) async-start(bf16[16,30,1024]{2,1,0:T(8,128)(2,1)} %get-tuple-element.6), calls=%async_computation.2 | async-start | bytes 2097152 | tf_op jit(solution)/shard_map/all_to_all | solution.py:64
  38.5 29.7 %copy-start.7 = (bf16[1,512,256]{2,1,0:T(8,128)(2,1)S(1)}, bf16[1,512,256]{2,1,0:T(8,128)(2,1)}, u32[]{:S(2)}) copy-start(bf16[1,512,256]{2,1,0:T(8,128)(2,1)} %param.17) | copy-start | bytes 786436
  38.5 65.1 %all-gather.6.cloned.1.call-start = ((), (), s32[]{:S(2)}) async-start(), calls=%async_computation.5 | async-start | bytes 2359296 | tf_op jit(solution)/shard_map/all_gather | solution.py:97
  63.4 29.7 %all-to-all-start = ((bf16[16,30,1024]{2,1,0:T(8,128)(2,1)}), bf16[16,30,1024]{2,1,0:T(8,128)(2,1)S(1)}, u32[]{:S(2)}, u32[]{:S(2)}) async-start(bf16[16,30,1024]{2,1,0:T(8,128)(2,1)} %get-tuple-element.7), calls=%async_computation | async-start | bytes 2097152 | tf_op jit(solution)/shard_map/all_to_all | solution.py:71
  68.1 40.1 %all-gather.8.cloned.1.call-start = ((), (), s32[]{:S(2)}) async-start(), calls=%async_computation.6 | async-start | bytes 2359296 | tf_op jit(solution)/shard_map/all_gather | solution.py:97
  68.2 7.6 %collective-permute-start = (bf16[1,512,256]{2,1,0:T(8,128)(2,1)S(1)}, bf16[1,512,256]{2,1,0:T(8,128)(2,1)}, u32[]{:S(2)}, u32[]{:S(2)}) collective-permute-start(bf16[1,512,256]{2,1,0:T(8,128)(2,1)S(1)} %copy-done.7), channel_id=1, source_target_pairs={{0,16},{16,0},{1,17},{17,1},{2,18},{18,2},{3,19},{19,3},{4,20},{20... | collective-permute-start | bytes 786440 | tf_op jit(solution)/shard_map/ppermute | solution.py:12
  68.9 78.6 %reduce-scatter.2.cloned.1.call-start = ((), (), s32[]{:S(2)}) async-start(), calls=%async_computation.7 | async-start | bytes 3538944 | tf_op jit(solution)/shard_map/reduce_scatter | solution.py:106
  78.3 2.9 %copy-start.6 = (bf16[1024,256]{1,0:T(8,128)(2,1)}, bf16[1024,256]{1,0:T(8,128)(2,1)S(1)}, u32[]{:S(2)}) copy-start(bf16[1024,256]{1,0:T(8,128)(2,1)S(1)} %fusion.9) | copy-start | bytes 1572868
  93.4 3.9 %copy-start.3 = (bf16[480,1024]{1,0:T(8,128)(2,1)}, bf16[480,1024]{1,0:T(8,128)(2,1)S(1)}, u32[]{:S(2)}) copy-start(bf16[480,1024]{1,0:T(8,128)(2,1)S(1)} %reshape.91) | copy-start | bytes 2949124
  97.3 0.9 copy-start.4
  103.5 1.1 copy-start.5
  113.1 29.4 %all-to-all-start.1 = ((bf16[16,30,1024]{2,1,0:T(8,128)(2,1)}), bf16[16,30,1024]{2,1,0:T(8,128)(2,1)S(1)}, u32[]{:S(2)}, u32[]{:S(2)}) async-start(bf16[16,30,1024]{2,1,0:T(8,128)(2,1)} %reshape.92), calls=%async_computation.1 | async-start | bytes 2097152 | tf_op jit(solution)/shard_map/all_to_all | solution.py:107
Sparse Core Ops, SparseCore 0:
  9.5 27.2 all-gather.3
  40.8 26.6 all-gather.5
  70.5 26.6 all-gather.7
  103.6 33.0 reduce-scatter.1
